TPU v7x, 32 devices: a whole 2x2x4 slice. The times are simulated.
32 devices in a mesh: seq: 4 (over z), shard: 8 (over y, x, core).
Axes of the slice: x: 2, y: 2, z: 4, core: 2. Of those that a mesh axis runs over, the one named last changes fastest.
Arguments:
- tokens: bfloat16 [2, 8, 2048, 768], P(None, 'shard', 'seq'), may hold values from -6 to 6
- lengths: int32 [8, 2], P('shard'), may hold values from 512 to 2048, as said below
- w_qkv: bfloat16 [768, 2304], P('shard'), may hold values from -0.21875 to 0.21875
- b_query: bfloat16 [768], P('shard'), may hold values from -3 to 3
- b_value: bfloat16 [768], P('shard'), may hold values from -3 to 3
- w_out: bfloat16 [768, 768], P('shard'), may hold values from -6 to 6
- b_out: bfloat16 [768], P('shard'), may hold values from -3 to 3
- gain_one: bfloat16 [768], P('shard'), may hold values from 0.5 to 1.5
- shift_one: bfloat16 [768], P('shard'), may hold values from -3 to 3
- w_up: bfloat16 [768, 3072], P('shard'), may hold values from -0.21875 to 0.21875
- b_up: bfloat16 [3072], P('shard'), may hold values from -3 to 3
- w_down: bfloat16 [3072, 768], P('shard'), may hold values from -0.109375 to 0.109375
- b_down: bfloat16 [768], P('shard'), may hold values from -3 to 3
- gain_two: bfloat16 [768], P('shard'), may hold values from 0.5 to 1.5
- shift_two: bfloat16 [768], P('shard'), may hold values from -3 to 3
- cotangent: bfloat16 [2, 8, 2048, 768], P(None, 'shard', 'seq'), may hold values from -6 to 6
Outputs:
- layer_out: bfloat16 [2, 8, 2048, 768], P(None, 'shard', 'seq')
- input_grad: bfloat16 [2, 8, 2048, 768], P(None, 'shard', 'seq')
- grad_w_qkv: float32 [768, 2304], P('shard')
- grad_b_query: float32 [768], P('shard')
- grad_b_value: float32 [768], P('shard')
- grad_w_out: float32 [768, 768], P('shard')
- grad_b_out: float32 [768], P('shard')
- grad_gain_one: float32 [768], P('shard')
- grad_shift_one: float32 [768], P('shard')
- grad_w_up: float32 [768, 3072], P('shard')
- grad_b_up: float32 [3072], P('shard')
- grad_w_down: float32 [3072, 768], P('shard')
- grad_b_down: float32 [768], P('shard')
- grad_gain_two: float32 [768], P('shard')
- grad_shift_two: float32 [768], P('shard')
Inputs may be any that keep to these rules, and one draw needn't show every extreme that they name: `lengths`: each group's sequence in each micro-batch has this many valid tokens at the start of its 2048 slots; some entry equals 2048.
All inputs are finite; a program needn't handle non-finite values.
Results may differ from a plain program's by a relative error of at most 0.015.
Values may be sent and summed in bfloat16 or wider, within the bound.
A program may use at most 192 MiB of HBM per device.

v0:
```python
import math
import jax
import jax.numpy as jnp
from jax import lax
from jax.sharding import PartitionSpec as P

H = 12
norm_eps = 1e-06


def layer_norm(inputs, scales, shifts):
    centre = jnp.mean(inputs, axis=-1, keepdims=True)
    centred = inputs - centre
    spread = jnp.mean(centred * centred, axis=-1, keepdims=True)
    return centred * lax.rsqrt(spread + norm_eps) * scales + shifts


def gelu_exact(inputs):
    return jax.nn.gelu(inputs, approximate=False)


def matmul_plain(left, right):
    return jnp.dot(left, right, preferred_element_type=jnp.float32)


def matmul_left_t(left, right):
    return lax.dot_general(
        left, right, (((0,), (0,)), ((), ())), preferred_element_type=jnp.float32
    )


def matmul_right_t(left, right):
    return lax.dot_general(
        left, right, (((1,), (1,)), ((), ())), preferred_element_type=jnp.float32
    )


def fetch_forward(
    w_qkv,
    b_query,
    b_value,
    w_out,
    b_out,
    gain_one,
    shift_one,
    w_up,
    b_up,
    w_down,
    b_down,
    gain_two,
    shift_two,
):
    return (
        lax.all_gather(w_qkv, "shard", axis=0, tiled=True),
        lax.all_gather(b_query, "shard", axis=0, tiled=True),
        lax.all_gather(b_value, "shard", axis=0, tiled=True),
        lax.all_gather(w_out, "shard", axis=0, tiled=True),
        lax.all_gather(b_out, "shard", axis=0, tiled=True),
        lax.all_gather(gain_one, "shard", axis=0, tiled=True),
        lax.all_gather(shift_one, "shard", axis=0, tiled=True),
        lax.all_gather(w_up, "shard", axis=0, tiled=True),
        lax.all_gather(b_up, "shard", axis=0, tiled=True),
        lax.all_gather(w_down, "shard", axis=0, tiled=True),
        lax.all_gather(b_down, "shard", axis=0, tiled=True),
        lax.all_gather(gain_two, "shard", axis=0, tiled=True),
        lax.all_gather(shift_two, "shard", axis=0, tiled=True),
    )


def fetch_backward(
    w_qkv,
    b_query,
    b_value,
    w_out,
    b_out,
    gain_one,
    shift_one,
    w_up,
    b_up,
    w_down,
    b_down,
    gain_two,
    shift_two,
):
    return (
        lax.all_gather(w_qkv, "shard", axis=0, tiled=True),
        lax.all_gather(b_query, "shard", axis=0, tiled=True),
        lax.all_gather(b_value, "shard", axis=0, tiled=True),
        lax.all_gather(w_out, "shard", axis=0, tiled=True),
        lax.all_gather(b_out, "shard", axis=0, tiled=True),
        lax.all_gather(gain_one, "shard", axis=0, tiled=True),
        lax.all_gather(shift_one, "shard", axis=0, tiled=True),
        lax.all_gather(w_up, "shard", axis=0, tiled=True),
        lax.all_gather(b_up, "shard", axis=0, tiled=True),
        lax.all_gather(w_down, "shard", axis=0, tiled=True),
        lax.all_gather(b_down, "shard", axis=0, tiled=True),
        lax.all_gather(gain_two, "shard", axis=0, tiled=True),
        lax.all_gather(shift_two, "shard", axis=0, tiled=True),
    )


def attention_forward(qkv_heads, seq_length):
    seq_slots, _, head_count, head_dim = qkv_heads.shape
    scaling = 1.0 / math.sqrt(head_dim)
    block_rows = min(512, seq_slots)
    queries = qkv_heads[:, 0].reshape(seq_slots // block_rows, block_rows, head_count, head_dim)
    key_rows = qkv_heads[:, 1]
    value_rows = qkv_heads[:, 2]
    key_valid = jnp.arange(seq_slots, dtype=jnp.int32) < seq_length

    def one_block(q_block):
        scores = (
            jnp.einsum("qhd,khd->hqk", q_block, key_rows, preferred_element_type=jnp.float32)
            * scaling
        )
        scores = jnp.where(key_valid[None, None, :], scores, -1e30)
        row_max = jnp.max(scores, axis=-1, keepdims=True)
        row_sum = jnp.sum(jnp.exp(scores - row_max), axis=-1, keepdims=True)
        log_total = row_max + jnp.log(row_sum)
        probs = jnp.exp(scores - log_total).astype(jnp.bfloat16)
        context = jnp.einsum("hqk,khd->qhd", probs, value_rows, preferred_element_type=jnp.float32)
        return (context.astype(jnp.bfloat16), log_total[..., 0])

    context, log_total = lax.map(one_block, queries)
    return (context.reshape(seq_slots, head_count * head_dim), log_total)


def attention_backward(qkv_heads, log_total, grad_context, seq_length):
    seq_slots, _, head_count, head_dim = qkv_heads.shape
    scaling = 1.0 / math.sqrt(head_dim)
    block_rows = min(512, seq_slots)
    block_count = seq_slots // block_rows
    queries = qkv_heads[:, 0].reshape(block_count, block_rows, head_count, head_dim)
    key_rows = qkv_heads[:, 1]
    value_rows = qkv_heads[:, 2]
    grad_blocks = grad_context.reshape(block_count, block_rows, head_count, head_dim)
    key_valid = jnp.arange(seq_slots, dtype=jnp.int32) < seq_length

    def one_block(carried, block_item):
        key_grad, value_grad = carried
        q_block, log_block, grad_block = block_item
        scores = (
            jnp.einsum("qhd,khd->hqk", q_block, key_rows, preferred_element_type=jnp.float32)
            * scaling
        )
        scores = jnp.where(key_valid[None, None, :], scores, -1e30)
        probs = jnp.exp(scores - log_block[..., None])
        grad_probs = jnp.einsum(
            "qhd,khd->hqk", grad_block, value_rows, preferred_element_type=jnp.float32
        )
        row_dot = jnp.sum(probs * grad_probs, axis=-1, keepdims=True)
        grad_scores = (probs * (grad_probs - row_dot)).astype(jnp.bfloat16)
        query_grad = (
            jnp.einsum("hqk,khd->qhd", grad_scores, key_rows, preferred_element_type=jnp.float32)
            * scaling
        )
        key_grad = (
            key_grad
            + jnp.einsum("hqk,qhd->khd", grad_scores, q_block, preferred_element_type=jnp.float32)
            * scaling
        )
        value_grad = value_grad + jnp.einsum(
            "hqk,qhd->khd",
            probs.astype(jnp.bfloat16),
            grad_block,
            preferred_element_type=jnp.float32,
        )
        return ((key_grad, value_grad), query_grad)

    zero_acc = jnp.zeros((seq_slots, head_count, head_dim), jnp.float32)
    (key_grad, value_grad), query_grad = lax.scan(
        one_block, (zero_acc, zero_acc), (queries, log_total, grad_blocks)
    )
    query_grad = query_grad.reshape(seq_slots, head_count, head_dim)
    return jnp.stack([query_grad, key_grad, value_grad], axis=1).astype(jnp.bfloat16)


def on_device(
    tokens,
    lengths,
    w_qkv,
    b_query,
    b_value,
    w_out,
    b_out,
    gain_one,
    shift_one,
    w_up,
    b_up,
    w_down,
    b_down,
    gain_two,
    shift_two,
    cotangent,
):
    micro_count = tokens.shape[0]
    tok_rows = tokens.shape[2]
    width = tokens.shape[3]
    seq_devices = lax.axis_size("seq")
    seq_place = lax.axis_index("seq")
    shard_count = lax.axis_size("shard")
    head_local = H // seq_devices
    head_dim = width // H
    seq_slots = tok_rows * seq_devices
    positions = seq_place * tok_rows + jnp.arange(tok_rows, dtype=jnp.int32)
    shards = (
        w_qkv,
        b_query,
        b_value,
        w_out,
        b_out,
        gain_one,
        shift_one,
        w_up,
        b_up,
        w_down,
        b_down,
        gain_two,
        shift_two,
    )
    grad_sums = [
        jnp.zeros((piece.shape[0] * shard_count,) + piece.shape[1:], jnp.float32)
        for piece in shards
    ]
    outputs = []
    input_grads = []
    for current in range(micro_count):
        weights_full = fetch_forward(*shards)
        (
            qkv_matrix,
            query_bias,
            value_bias,
            out_matrix,
            out_bias,
            gain_first,
            shift_first,
            up_matrix,
            up_bias,
            down_matrix,
            down_bias,
            gain_second,
            shift_second,
        ) = weights_full
        inputs_mb = tokens[current, 0]
        seq_length = lengths[0, current]
        row_valid = (positions < seq_length).astype(jnp.float32)[:, None]
        bias_all = jnp.concatenate([query_bias, jnp.zeros_like(query_bias), value_bias]).astype(
            jnp.float32
        )
        projected = (matmul_plain(inputs_mb, qkv_matrix) + bias_all).astype(jnp.bfloat16)
        qkv_heads = lax.all_to_all(
            projected.reshape(tok_rows, 3, seq_devices, head_local * head_dim),
            "seq",
            split_axis=2,
            concat_axis=0,
            tiled=True,
        )
        qkv_heads = qkv_heads.reshape(seq_slots, 3, head_local, head_dim)
        context_heads, log_total = attention_forward(qkv_heads, seq_length)
        context = lax.all_to_all(context_heads, "seq", split_axis=0, concat_axis=1, tiled=True)
        gain_first_f = gain_first.astype(jnp.float32)
        shift_first_f = shift_first.astype(jnp.float32)
        gain_second_f = gain_second.astype(jnp.float32)
        shift_second_f = shift_second.astype(jnp.float32)
        residual_one = (
            inputs_mb.astype(jnp.float32)
            + matmul_plain(context, out_matrix)
            + out_bias.astype(jnp.float32)
        )
        hidden_one = layer_norm(residual_one, gain_first_f, shift_first_f)
        hidden_low = hidden_one.astype(jnp.bfloat16)
        up_proj = matmul_plain(hidden_low, up_matrix) + up_bias.astype(jnp.float32)
        activated = gelu_exact(up_proj).astype(jnp.bfloat16)
        residual_two = (
            hidden_one + matmul_plain(activated, down_matrix) + down_bias.astype(jnp.float32)
        )
        outputs.append(layer_norm(residual_two, gain_second_f, shift_second_f).astype(jnp.bfloat16))
        weights_full = fetch_backward(*shards)
        (
            qkv_matrix,
            query_bias,
            value_bias,
            out_matrix,
            out_bias,
            gain_first,
            shift_first,
            up_matrix,
            up_bias,
            down_matrix,
            down_bias,
            gain_second,
            shift_second,
        ) = weights_full
        out_grad = cotangent[current, 0].astype(jnp.float32) * row_valid
        _, back_second = jax.vjp(layer_norm, residual_two, gain_second_f, shift_second_f)
        grad_residual_two, grad_gain_second, grad_shift_second = back_second(out_grad)
        down_grad = grad_residual_two.astype(jnp.bfloat16)
        grad_down = matmul_left_t(activated, down_grad)
        grad_down_bias = jnp.sum(down_grad.astype(jnp.float32), axis=0)
        _, back_gelu = jax.vjp(gelu_exact, up_proj)
        (grad_up_proj,) = back_gelu(matmul_right_t(down_grad, down_matrix))
        up_grad = grad_up_proj.astype(jnp.bfloat16)
        grad_up = matmul_left_t(hidden_low, up_grad)
        grad_up_bias = jnp.sum(up_grad.astype(jnp.float32), axis=0)
        grad_hidden_one = grad_residual_two + matmul_right_t(up_grad, up_matrix)
        _, back_first = jax.vjp(layer_norm, residual_one, gain_first_f, shift_first_f)
        grad_residual_one, grad_gain_first, grad_shift_first = back_first(grad_hidden_one)
        attn_grad = grad_residual_one.astype(jnp.bfloat16)
        grad_out = matmul_left_t(context, attn_grad)
        grad_out_bias = jnp.sum(attn_grad.astype(jnp.float32), axis=0)
        context_grad = matmul_right_t(attn_grad, out_matrix).astype(jnp.bfloat16)
        grad_heads = lax.all_to_all(context_grad, "seq", split_axis=1, concat_axis=0, tiled=True)
        grad_heads = grad_heads.reshape(seq_slots, head_local, head_dim)
        qkv_head_grad = attention_backward(qkv_heads, log_total, grad_heads, seq_length)
        qkv_grad = lax.all_to_all(
            qkv_head_grad.reshape(seq_slots, 3, 1, head_local * head_dim),
            "seq",
            split_axis=0,
            concat_axis=2,
            tiled=True,
        )
        qkv_grad = qkv_grad.reshape(tok_rows, 3 * width)
        grad_qkv = matmul_left_t(inputs_mb, qkv_grad)
        bias_grad_all = jnp.sum(qkv_grad.astype(jnp.float32), axis=0)
        input_grads.append(
            (grad_residual_one + matmul_right_t(qkv_grad, qkv_matrix)).astype(jnp.bfloat16)
        )
        terms = (
            grad_qkv,
            bias_grad_all[:width],
            bias_grad_all[2 * width :],
            grad_out,
            grad_out_bias,
            grad_gain_first,
            grad_shift_first,
            grad_up,
            grad_up_bias,
            grad_down,
            grad_down_bias,
            grad_gain_second,
            grad_shift_second,
        )
        grad_sums = [total + term for total, term in zip(grad_sums, terms)]
    shard_sums = (
        lax.psum_scatter(grad_sums[0], "shard", scatter_dimension=0, tiled=True),
        lax.psum_scatter(grad_sums[1], "shard", scatter_dimension=0, tiled=True),
        lax.psum_scatter(grad_sums[2], "shard", scatter_dimension=0, tiled=True),
        lax.psum_scatter(grad_sums[3], "shard", scatter_dimension=0, tiled=True),
        lax.psum_scatter(grad_sums[4], "shard", scatter_dimension=0, tiled=True),
        lax.psum_scatter(grad_sums[5], "shard", scatter_dimension=0, tiled=True),
        lax.psum_scatter(grad_sums[6], "shard", scatter_dimension=0, tiled=True),
        lax.psum_scatter(grad_sums[7], "shard", scatter_dimension=0, tiled=True),
        lax.psum_scatter(grad_sums[8], "shard", scatter_dimension=0, tiled=True),
        lax.psum_scatter(grad_sums[9], "shard", scatter_dimension=0, tiled=True),
        lax.psum_scatter(grad_sums[10], "shard", scatter_dimension=0, tiled=True),
        lax.psum_scatter(grad_sums[11], "shard", scatter_dimension=0, tiled=True),
        lax.psum_scatter(grad_sums[12], "shard", scatter_dimension=0, tiled=True),
    )
    summed = (
        lax.psum(shard_sums[0].astype(jnp.bfloat16), "seq").astype(jnp.float32),
        lax.psum(shard_sums[1].astype(jnp.bfloat16), "seq").astype(jnp.float32),
        lax.psum(shard_sums[2].astype(jnp.bfloat16), "seq").astype(jnp.float32),
        lax.psum(shard_sums[3].astype(jnp.bfloat16), "seq").astype(jnp.float32),
        lax.psum(shard_sums[4].astype(jnp.bfloat16), "seq").astype(jnp.float32),
        lax.psum(shard_sums[5].astype(jnp.bfloat16), "seq").astype(jnp.float32),
        lax.psum(shard_sums[6].astype(jnp.bfloat16), "seq").astype(jnp.float32),
        lax.psum(shard_sums[7].astype(jnp.bfloat16), "seq").astype(jnp.float32),
        lax.psum(shard_sums[8].astype(jnp.bfloat16), "seq").astype(jnp.float32),
        lax.psum(shard_sums[9].astype(jnp.bfloat16), "seq").astype(jnp.float32),
        lax.psum(shard_sums[10].astype(jnp.bfloat16), "seq").astype(jnp.float32),
        lax.psum(shard_sums[11].astype(jnp.bfloat16), "seq").astype(jnp.float32),
        lax.psum(shard_sums[12].astype(jnp.bfloat16), "seq").astype(jnp.float32),
    )
    layer_out = jnp.stack(outputs, axis=0)[:, None]
    input_grad = jnp.stack(input_grads, axis=0)[:, None]
    return (
        layer_out,
        input_grad,
        summed[0],
        summed[1],
        summed[2],
        summed[3],
        summed[4],
        summed[5],
        summed[6],
        summed[7],
        summed[8],
        summed[9],
        summed[10],
        summed[11],
        summed[12],
    )


def solution(mesh):
    placed = (
        P(None, "shard", "seq", None),
        P("shard", None),
        P("shard", None),
        P("shard"),
        P("shard"),
        P("shard", None),
        P("shard"),
        P("shard"),
        P("shard"),
        P("shard", None),
        P("shard"),
        P("shard", None),
        P("shard"),
        P("shard"),
        P("shard"),
        P(None, "shard", "seq", None),
    )
    return jax.shard_map(
        on_device,
        mesh=mesh,
        in_specs=placed,
        out_specs=(
            P(None, "shard", "seq", None),
            P(None, "shard", "seq", None),
            P("shard", None),
            P("shard"),
            P("shard"),
            P("shard", None),
            P("shard"),
            P("shard"),
            P("shard"),
            P("shard", None),
            P("shard"),
            P("shard", None),
            P("shard"),
            P("shard"),
            P("shard"),
        ),
        check_vma=False,
    )
```

profile of v0, /device:TPU:0, one launch (start us, length us, event | category | flops | bytes accessed | tf_op | source)
XLA Modules:
  0.0 961.6 jit_solution(3195086936663808667)
XLA Ops:
  16.6 27.1 %all-reduce.18 = (bf16[768]{0:T(1024)(128)(2,1)S(1)}, bf16[768]{0:T(1024)(128)(2,1)S(1)}, bf16[768]{0:T(1024)(128)(2,1)}, bf16[768]{0:T(1024)(128)(2,1)}, bf16[7...) all-reduce(bf16[768]{0:T(1024)(128)(2,1)S(1)} %dynamic-update-slice, ...), channel_id=1, replica_groups=mesh['seq'=4,'shard'=8] {'shard'}, use_global_device_ids=true, to_apply=%add.1 | all-reduce | flops 6144 | bytes 24576
  46.7 5.7 fusion.104
  63.7 5.6 fusion.105
  76.9 39.0 %all-to-all-done = bf16[512,3,4,192]{0,3,1,2:T(8,128)(2,1)S(1)} async-done(((bf16[512,3,4,192]{0,3,1,2:T(8,128)(2,1)}), bf16[512,3,4,192]{0,3,1,2:T(8,128)(2,1)S(1)}, u32[]{:S(2)}, u32[]{:S(2)}) %all-to-all-start) | async-done | bytes 2359328 | tf_op jit(solution)/shard_map/all_to_all | solution.py:251
  123.9 5.9 reshape.403
  133.3 36.4 %while.56 = (s32[]{:T(128)}, bf16[4,512,3,64]{1,3,2,0:T(8,128)(2,1)}, f32[4,3,512]{2,1,0:T(4,128)S(1)}, bf16[4,512,3,64]{1,3,2,0:T(8,128)(2,1)S(1)}, bf16[2048,3...) while((s32[]{:T(128)}, ...), condition=%wide.region_3.4_spmd.clone, body=%wide.region_0.3_spmd.clone.sunk | while | flops 840008192 | bytes 39780960 | solution.py:124
  183.8 5.9 reshape.405
  192.3 34.0 %while.57 = (s32[]{:T(128)}, bf16[4,512,3,64]{1,3,2,0:T(8,128)(2,1)S(1)}, f32[4,3,512]{2,1,0:T(4,128)S(1)}, bf16[4,512,3,64]{1,3,2,0:T(8,128)(2,1)S(1)}, bf16[20...) while((s32[]{:T(128)}, ...), condition=%wide.region_11.12_spmd.clone, body=%wide.region_8.11_spmd.clone.sunk | while | flops 840008192 | bytes 39782500 | solution.py:124
  227.2 5.1 all-to-all-start.3
  232.9 8.8 all-gather
  255.2 5.0 fusion.144
  262.9 34.8 %multiply_convert_fusion.3 = (bf16[512,3072]{1,0:T(8,128)(2,1)}, f32[512,3072]{1,0:T(8,128)}, bf16[512,3072]{1,0:T(8,128)(2,1)}, f32[512,3072]{1,0:T(8,128)}, f32[512,3072]{1,0:T(8,128)}) fusion(f32[3072]{0:T(1024)S(1)} %bitcast.336, f32[512,3072]{1,0:T(8,128)S(1)} %fusion.144, bf16[768,3072]{1,0:T(8,128)(2,1)S(1)} %copy-done.66, ...), kind=kOutput, calls=%fused_computation.126 | convolution fusion | flops 2625503232 | bytes 37771264 | tf_op jit(solution)/shard_map/dot_general | solution.py:23
  297.6 6.2 fusion.161
  320.2 18.1 %convert_reduce_fusion.1 = (f32[3072]{0:T(1024)}, bf16[512,3072]{1,0:T(8,128)(2,1)}, f32[3072]{0:T(1024)}, bf16[512,3072]{1,0:T(8,128)(2,1)}) fusion(f32[512,3072]{1,0:T(8,128)} %get-tuple-element.761, f32[512,3072]{1,0:T(8,128)} %get-tuple-element.802, f32[3072]{0:T(1024)S(1)} %bitcast.337, f32[512,3072]{1,0:T(8,128)} %fusion.162, ...), kind=kOutput, calls=%fused_computation.110 | convolution fusion | flops 2469390336 | bytes 43290624 | tf_op jit(solution)/shard_map/dot_general | solution.py:33
  338.3 6.1 add_add_fusion.8
  344.4 6.4 multiply_reduce_fusion.3
  364.8 5.3 convolution_add_fusion
  380.0 9.0 fusion.146
  393.0 8.9 convolution_add_fusion.1
  401.9 5.3 all-to-all-start.6
  408.2 124.5 %while.58 = (s32[]{:T(128)}, f32[2048,3,64]{0,2,1:T(8,128)S(1)}, f32[2048,3,64]{0,2,1:T(8,128)}, bf16[4,512,3,64]{1,3,2,0:T(8,128)(2,1)}, bf16[4,512,3,64]{1,3,2...) while((s32[]{:T(128)}, f32[2048,3,64]{0,2,1:T(8,128)S(1)}, ...), condition=%wide.region_22.23_spmd.clone, body=%wide.region_20.22_spmd.clone.sunk | while | flops 2062516736 | bytes 204919504 | solution.py:171
  427.4 7.0 fusion.273
  458.0 6.4 fusion.273
  464.4 5.6 fusion.272
  488.6 7.4 fusion.273
  496.0 5.9 fusion.272
  520.7 6.4 fusion.273
  527.2 5.5 fusion.272
  541.7 5.8 all-to-all-start.5
  548.5 120.6 %while.59 = (s32[]{:T(128)}, f32[2048,3,64]{0,2,1:T(8,128)S(1)}, f32[2048,3,64]{0,2,1:T(8,128)}, bf16[4,512,3,64]{1,3,2,0:T(8,128)(2,1)}, bf16[4,512,3,64]{1,3,2...) while((s32[]{:T(128)}, f32[2048,3,64]{0,2,1:T(8,128)S(1)}, ...), condition=%wide.region_29.30_spmd.clone, body=%wide.region_27.29_spmd.clone.sunk | while | flops 2062516736 | bytes 204919504 | solution.py:171
  567.1 6.3 fusion.286
  596.8 6.3 fusion.286
  603.0 5.5 fusion.285
  627.1 6.3 fusion.286
  633.3 5.5 fusion.285
  657.4 6.3 fusion.286
  663.6 5.5 fusion.285
  678.1 5.2 all-to-all-start.7
  683.3 7.8 copy.160
  691.1 81.0 %all-to-all-done.7 = bf16[2048,3,1,192]{3,1,2,0:T(4,128)(2,1)} async-done(((bf16[2048,3,1,192]{3,1,2,0:T(4,128)(2,1)}), bf16[2048,3,1,192]{3,1,2,0:T(4,128)(2,1)}, u32[]{:S(2)}, u32[]{:S(2)}) %all-to-all-start.7) | async-done | bytes 2359328 | tf_op jit(solution)/shard_map/all_to_all | solution.py:315
  772.1 7.2 copy.161
  786.2 5.0 add_bitcast_fusion
  791.1 8.0 copy.162
  812.9 50.6 %reduce-scatter.13.cloned.1.call-done = f32[96,2304]{1,0:T(8,128)} async-done(((f32[768,2304]{1,0:T(8,128)}), f32[96,2304]{1,0:T(8,128)}) %reduce-scatter.13.cloned.1.call-update) | async-done | bytes 884752
  867.2 24.6 %all-reduce.17 = (bf16[768]{0:T(1024)(128)(2,1)S(1)}, bf16[768]{0:T(1024)(128)(2,1)S(1)}, bf16[768]{0:T(1024)(128)(2,1)S(1)}, bf16[768]{0:T(1024)(128)(2,1)S(1)}...) all-reduce(f32[768]{0:T(1024)S(1)} %add.360, ...), channel_id=3, replica_groups=mesh['seq'=4,'shard'=8] {'shard'}, use_global_device_ids=true, to_apply=%region_34.35.clone | all-reduce | flops 9216 | bytes 55296
  892.5 12.8 %all-reduce.19 = (bf16[96]{0:T(256)(128)(2,1)S(1)}, bf16[96]{0:T(256)(128)(2,1)S(1)}, bf16[96]{0:T(256)(128)(2,1)S(1)}, bf16[96]{0:T(256)(128)(2,1)S(1)}, bf16[9...) all-reduce(bf16[96]{0:T(256)(128)(2,1)S(1)} %dynamic-slice.43, ...), channel_id=1, replica_groups=mesh['seq'=4,'shard'=8] {'seq'}, use_global_device_ids=true, to_apply=%region_35.36 | all-reduce | flops 1152 | bytes 4608 | tf_op jit(solution)/shard_map/psum | solution.py:361
  910.0 5.4 fusion.120
  919.1 29.5 %all-reduce.23.cloned.1.call-done = (bf16[96,2304]{0,1:T(8,128)(2,1)}, bf16[96,768]{1,0:T(8,128)(2,1)}, bf16[96,3072]{1,0:T(8,128)(2,1)}, bf16[384,768]{1,0:T(8,128)(2,1)}) async-done(((bf16[96,2304]{0,1:T(8,128)(2,1)}, bf16[96,768]{1,0:T(8,128)(2,1)}, bf16[96,3072]{1,0:T(8,128)(2,1)}, bf16[384,768]{1,0:T(8,128)(2,1)}), (bf16[96,2304]{0,1:T(8,128)(2,1)}, bf16[96,768]{1,0:T(8,128)(2,1)}, ...) | async-done | bytes 1769488 | tf_op jit(solution)/shard_map/psum | solution.py:360
  (441 shorter events, 406.6 us)
Async XLA Ops:
  7.2 39.5 %all-gather.6.cloned.1.call-start = ((), (), s32[]{:S(2)}) async-start(), calls=%async_computation.12 | async-start | bytes 3981312 | tf_op jit(solution)/shard_map/all_gather | solution.py:54
  56.9 59.0 %all-to-all-start = ((bf16[512,3,4,192]{0,3,1,2:T(8,128)(2,1)}), bf16[512,3,4,192]{0,3,1,2:T(8,128)(2,1)S(1)}, u32[]{:S(2)}, u32[]{:S(2)}) async-start(bf16[512,3,4,192]{0,3,1,2:T(8,128)(2,1)} %copy.136), calls=%async_computation | async-start | bytes 4718592 | tf_op jit(solution)/shard_map/all_to_all | solution.py:251
  61.7 181.5 %all-gather.8.cloned.1.call-start = ((), (), s32[]{:S(2)}) async-start(), calls=%async_computation.13 | async-start | bytes 1327104 | tf_op jit(solution)/shard_map/all_gather | solution.py:57
  62.4 192.8 %all-gather.10.cloned.1.call-start = ((), (), s32[]{:S(2)}) async-start(), calls=%async_computation.14 | async-start | bytes 5308416 | tf_op jit(solution)/shard_map/all_gather | solution.py:61
  115.9 58.2 %all-to-all-start.2 = ((bf16[512,3,4,192]{0,3,1,2:T(8,128)(2,1)}), bf16[512,3,4,192]{0,3,1,2:T(8,128)(2,1)}, u32[]{:S(2)}, u32[]{:S(2)}) async-start(bf16[512,3,4,192]{0,3,1,2:T(8,128)(2,1)} %copy.140), calls=%async_computation.2 | async-start | bytes 4718592 | tf_op jit(solution)/shard_map/all_to_all | solution.py:251
  169.7 14.1 %copy-start.6 = (bf16[2048,3,64]{0,2,1:T(8,128)(2,1)}, bf16[2048,3,64]{0,2,1:T(8,128)(2,1)S(1)}, u32[]{:S(2)}) copy-start(bf16[2048,3,64]{0,2,1:T(8,128)(2,1)S(1)} %get-tuple-element.1181) | copy-start | bytes 2359300
  169.7 14.1 %copy-start.11 = (bf16[2048,3,64]{0,2,1:T(8,128)(2,1)}, bf16[2048,3,64]{0,2,1:T(8,128)(2,1)S(1)}, u32[]{:S(2)}) copy-start(bf16[2048,3,64]{0,2,1:T(8,128)(2,1)S(1)} %get-tuple-element.1187) | copy-start | bytes 2359300
  169.7 14.1 %copy-start.14 = (bf16[4,512,3,64]{1,3,2,0:T(8,128)(2,1)}, bf16[4,512,3,64]{1,3,2,0:T(8,128)(2,1)S(1)}, u32[]{:S(2)}) copy-start(bf16[4,512,3,64]{1,3,2,0:T(8,128)(2,1)S(1)} %get-tuple-element.1191) | copy-start | bytes 2359300
  169.7 14.1 %copy-start.37 = (f32[4,3,512]{2,1,0:T(4,128)}, f32[4,3,512]{2,1,0:T(4,128)S(1)}, u32[]{:S(2)}) copy-start(f32[4,3,512]{2,1,0:T(4,128)S(1)} %get-tuple-element.1134) | copy-start | bytes 73732
  174.1 52.2 %all-to-all-start.1 = ((bf16[4,512,192]{1,2,0:T(8,128)(2,1)}), bf16[4,512,192]{1,2,0:T(8,128)(2,1)}, u32[]{:S(2)}, u32[]{:S(2)}) async-start(bf16[4,512,192]{1,2,0:T(8,128)(2,1)} %bitcast.8), calls=%async_computation.1 | async-start | bytes 1572864 | tf_op jit(solution)/shard_map/all_to_all | solution.py:260
  192.2 40.6 %copy-start.63 = (bf16[768]{0:T(1024)(128)(2,1)S(1)}, bf16[768]{0:T(1024)(128)(2,1)}, u32[]{:S(2)}) copy-start(bf16[768]{0:T(1024)(128)(2,1)} %get-tuple-element.717) | copy-start | bytes 4612
  192.2 40.6 %copy-start.62 = (bf16[768]{0:T(1024)(128)(2,1)S(1)}, bf16[768]{0:T(1024)(128)(2,1)}, u32[]{:S(2)}) copy-start(bf16[768]{0:T(1024)(128)(2,1)} %get-tuple-element.719) | copy-start | bytes 4612
  192.3 40.6 %copy-start.61 = (bf16[768]{0:T(1024)(128)(2,1)S(1)}, bf16[768]{0:T(1024)(128)(2,1)}, u32[]{:S(2)}) copy-start(bf16[768]{0:T(1024)(128)(2,1)} %get-tuple-element.718) | copy-start | bytes 4612
  192.3 40.6 %copy-start.65 = (bf16[384]{0:T(512)(128)(2,1)S(1)}, bf16[384]{0:T(512)(128)(2,1)}, u32[]{:S(2)}) copy-start(bf16[384]{0:T(512)(128)(2,1)} %param.34) | copy-start | bytes 2308
  192.3 49.5 %copy-start.60 = (bf16[768]{0:T(1024)(128)(2,1)S(1)}, bf16[768]{0:T(1024)(128)(2,1)}, u32[]{:S(2)}) copy-start(bf16[768]{0:T(1024)(128)(2,1)} %get-tuple-element.720) | copy-start | bytes 4612
  192.3 49.5 %copy-start.59 = (bf16[768]{0:T(1024)(128)(2,1)S(1)}, bf16[768]{0:T(1024)(128)(2,1)}, u32[]{:S(2)}) copy-start(bf16[768]{0:T(1024)(128)(2,1)} %get-tuple-element.721) | copy-start | bytes 4612
  192.3 49.5 %copy-start.58 = (bf16[768]{0:T(1024)(128)(2,1)S(1)}, bf16[768]{0:T(1024)(128)(2,1)}, u32[]{:S(2)}) copy-start(bf16[768]{0:T(1024)(128)(2,1)} %get-tuple-element.722) | copy-start | bytes 4612
  226.3 20.7 %copy-start.4 = (bf16[2048,3,64]{0,2,1:T(8,128)(2,1)}, bf16[2048,3,64]{0,2,1:T(8,128)(2,1)S(1)}, u32[]{:S(2)}) copy-start(bf16[2048,3,64]{0,2,1:T(8,128)(2,1)S(1)} %get-tuple-element.1180) | copy-start | bytes 2359300
  226.3 20.7 %copy-start.9 = (bf16[2048,3,64]{0,2,1:T(8,128)(2,1)}, bf16[2048,3,64]{0,2,1:T(8,128)(2,1)S(1)}, u32[]{:S(2)}) copy-start(bf16[2048,3,64]{0,2,1:T(8,128)(2,1)S(1)} %get-tuple-element.1186) | copy-start | bytes 2359300
  226.3 20.7 %copy-start.13 = (bf16[4,512,3,64]{1,3,2,0:T(8,128)(2,1)}, bf16[4,512,3,64]{1,3,2,0:T(8,128)(2,1)S(1)}, u32[]{:S(2)}) copy-start(bf16[4,512,3,64]{1,3,2,0:T(8,128)(2,1)S(1)} %get-tuple-element.1190) | copy-start | bytes 2359300
  226.3 20.7 %copy-start.38 = (f32[4,3,512]{2,1,0:T(4,128)}, f32[4,3,512]{2,1,0:T(4,128)S(1)}, u32[]{:S(2)}) copy-start(f32[4,3,512]{2,1,0:T(4,128)S(1)} %get-tuple-element.1098) | copy-start | bytes 73732
  227.2 24.2 %all-to-all-start.3 = ((bf16[4,512,192]{1,2,0:T(8,128)(2,1)}), bf16[4,512,192]{1,2,0:T(8,128)(2,1)S(1)}, u32[]{:S(2)}, u32[]{:S(2)}) async-start(bf16[4,512,192]{1,2,0:T(8,128)(2,1)} %bitcast.331), calls=%async_computation.3 | async-start | bytes 1572864 | tf_op jit(solution)/shard_map/all_to_all | solution.py:260
  232.2 65.4 %all-gather.12.cloned.1.call-start = ((), (), s32[]{:S(2)}) async-start(), calls=%async_computation.15 | async-start | bytes 5308416 | tf_op jit(solution)/shard_map/all_gather | solution.py:63
  232.8 570.6 %reduce-scatter.7.cloned.1.call-start = ((), (), s32[]{:S(2)}) async-start(), calls=%async_computation.16 | async-start | bytes 2654208 | tf_op jit(solution)/shard_map/reduce_scatter | solution.py:348
  255.2 7.6 copy-start.66
  359.9 448.4 %reduce-scatter.11.cloned.1.call-start = ((), (), s32[]{:S(2)}) async-start(), calls=%async_computation.18 | async-start | bytes 10616832 | tf_op jit(solution)/shard_map/reduce_scatter | solution.py:354
  375.7 26.2 %all-to-all-start.4 = ((bf16[512,4,192]{0,2,1:T(8,128)(2,1)}), bf16[512,4,192]{0,2,1:T(8,128)(2,1)}, u32[]{:S(2)}, u32[]{:S(2)}) async-start(bf16[512,4,192]{0,2,1:T(8,128)(2,1)} %bitcast.330), calls=%async_computation.4 | async-start | bytes 1572864 | tf_op jit(solution)/shard_map/all_to_all | solution.py:312
  379.9 430.7 %reduce-scatter.9.cloned.1.call-start = ((), (), s32[]{:S(2)}) async-start(), calls=%async_computation.17 | async-start | bytes 10616832 | tf_op jit(solution)/shard_map/reduce_scatter | solution.py:352
  380.0 9.0 copy-start.29
  380.0 9.0 copy-start.69
  401.9 139.8 %all-to-all-start.6 = ((bf16[512,4,192]{0,2,1:T(8,128)(2,1)}), bf16[512,4,192]{0,2,1:T(8,128)(2,1)}, u32[]{:S(2)}, u32[]{:S(2)}) async-start(bf16[512,4,192]{0,2,1:T(8,128)(2,1)} %bitcast.329), calls=%async_computation.6 | async-start | bytes 1572864 | tf_op jit(solution)/shard_map/all_to_all | solution.py:312
  411.0 7.1 copy-start
  423.0 11.4 %copy-start.1 = (f32[3,512,2048]{2,1,0:T(8,128)S(1)}, f32[3,512,2048]{2,1,0:T(8,128)}, u32[]{:S(2)}) copy-start(f32[3,512,2048]{2,1,0:T(8,128)} %copy-done) | copy-start | bytes 37748740 | tf_op jit(solution)/shard_map/while
  453.6 10.8 %copy-start.1 = (f32[3,512,2048]{2,1,0:T(8,128)S(1)}, f32[3,512,2048]{2,1,0:T(8,128)}, u32[]{:S(2)}) copy-start(f32[3,512,2048]{2,1,0:T(8,128)} %copy-done) | copy-start | bytes 37748740 | tf_op jit(solution)/shard_map/while
  484.1 11.9 %copy-start.1 = (f32[3,512,2048]{2,1,0:T(8,128)S(1)}, f32[3,512,2048]{2,1,0:T(8,128)}, u32[]{:S(2)}) copy-start(f32[3,512,2048]{2,1,0:T(8,128)} %copy-done) | copy-start | bytes 37748740 | tf_op jit(solution)/shard_map/while
  516.0 11.1 %copy-start.1 = (f32[3,512,2048]{2,1,0:T(8,128)S(1)}, f32[3,512,2048]{2,1,0:T(8,128)}, u32[]{:S(2)}) copy-start(f32[3,512,2048]{2,1,0:T(8,128)} %copy-done) | copy-start | bytes 37748740 | tf_op jit(solution)/shard_map/while
  541.7 6.8 copy-start.5
  541.7 6.8 copy-start.8
  541.7 6.8 copy-start.10
  541.7 136.4 %all-to-all-start.5 = ((bf16[2048,3,1,192]{3,1,2,0:T(4,128)(2,1)}), bf16[2048,3,1,192]{3,1,2,0:T(4,128)(2,1)}, u32[]{:S(2)}, u32[]{:S(2)}) async-start(bf16[2048,3,1,192]{3,1,2,0:T(4,128)(2,1)} %copy.146), calls=%async_computation.5 | async-start | bytes 8388608 | tf_op jit(solution)/shard_map/all_to_all | solution.py:315
  562.6 10.7 %copy-start.3 = (f32[3,512,2048]{2,1,0:T(8,128)S(1)}, f32[3,512,2048]{2,1,0:T(8,128)}, u32[]{:S(2)}) copy-start(f32[3,512,2048]{2,1,0:T(8,128)} %copy-done.2) | copy-start | bytes 37748740 | tf_op jit(solution)/shard_map/while
  592.4 10.7 %copy-start.3 = (f32[3,512,2048]{2,1,0:T(8,128)S(1)}, f32[3,512,2048]{2,1,0:T(8,128)}, u32[]{:S(2)}) copy-start(f32[3,512,2048]{2,1,0:T(8,128)} %copy-done.2) | copy-start | bytes 37748740 | tf_op jit(solution)/shard_map/while
  622.7 10.7 %copy-start.3 = (f32[3,512,2048]{2,1,0:T(8,128)S(1)}, f32[3,512,2048]{2,1,0:T(8,128)}, u32[]{:S(2)}) copy-start(f32[3,512,2048]{2,1,0:T(8,128)} %copy-done.2) | copy-start | bytes 37748740 | tf_op jit(solution)/shard_map/while
  653.0 10.7 %copy-start.3 = (f32[3,512,2048]{2,1,0:T(8,128)S(1)}, f32[3,512,2048]{2,1,0:T(8,128)}, u32[]{:S(2)}) copy-start(f32[3,512,2048]{2,1,0:T(8,128)} %copy-done.2) | copy-start | bytes 37748740 | tf_op jit(solution)/shard_map/while
  678.1 94.0 %all-to-all-start.7 = ((bf16[2048,3,1,192]{3,1,2,0:T(4,128)(2,1)}), bf16[2048,3,1,192]{3,1,2,0:T(4,128)(2,1)}, u32[]{:S(2)}, u32[]{:S(2)}) async-start(bf16[2048,3,1,192]{3,1,2,0:T(4,128)(2,1)} %copy.152), calls=%async_computation.7 | async-start | bytes 8388608 | tf_op jit(solution)/shard_map/all_to_all | solution.py:315
  683.3 180.2 %reduce-scatter.13.cloned.1.call-start = ((), (), s32[]{:S(2)}) async-start(), calls=%async_computation.19 | async-start | bytes 7962624
  799.3 149.2 %all-reduce.23.cloned.1.call-start = ((), (), s32[]{:S(2)}) async-start(), calls=%async_computation.20 | async-start | bytes 3833856 | tf_op jit(solution)/shard_map/psum | solution.py:360
  812.9 97.1 %copy-start.53 = (f32[512]{0:T(512)S(1)}, f32[512]{0:T(512)}, u32[]{:S(2)}) copy-start(f32[512]{0:T(512)} %copy-done.52) | copy-start | bytes 6148
  (54 other events, 204.4 us)
Sparse Core Ops, SparseCore 0:
  9.9 36.7 all-gather.5
  64.4 24.3 all-gather.7
  90.7 38.7 all-gather.9
  234.6 39.2 all-gather.11
  360.0 40.3 reduce-scatter.6
  403.8 76.8 reduce-scatter.10
  484.1 76.8 reduce-scatter.8
  799.4 64.0 reduce-scatter.12
  867.3 81.2 all-reduce.22
where the time goes:
time: 971 us; the launch traced here: 962 us
  matrix products  389 us (40%)
  waiting for transfers between devices  215 us (22%)
  other arithmetic  115 us (12%)
  local copies, waits for them, and re-layouts  112 us (12%)
  blocking collectives  73.4 us (8%)
  starting transfers between devices  40 us (4%)
  between operations  17.3 us (2%)
    all_to_all x2, waiting for transfers between devices, on_device(): lax.all_to_all(qkv_head_grad.reshape(seq_slots, 3, 1, head_local * head_d...  81 us
    dot_general x8, matrix products, matmul_plain(): return jnp.dot(left, right, preferred_element_type=jnp.float32)  66.5 us
    unnamed x10, waiting for transfers between devices  53.3 us
    dot_general x8, matrix products, one_block(): jnp.einsum('hqk,khd->qhd', grad_scores, key_rows, preferred_element_type=...  52.3 us
    unnamed x2, blocking collectives  51.8 us
    dot_general x8, matrix products, matmul_right_t(): lax.dot_general(left, right, (((1,), (1,)), ((), ())), preferred_element_...  47.5 us
    all_to_all x2, waiting for transfers between devices, on_device(): lax.all_to_all(projected.reshape(tok_rows, 3, seq_devices, head_local * h...  43.5 us
    dot_general x8, matrix products, one_block(): jnp.einsum('hqk,qhd->khd', probs.astype(jnp.bfloat16), grad_block, prefer...  43.4 us
  transfers between devices with their start and end apart: 17, of which 7 were waited for; matrix products, arithmetic and copies ran while one was open for 55% of the time, Pallas kernels for 0%

commit v1 on v0

--- a/solution.py
+++ b/solution.py
@@ -312,12 +312,20 @@
         grad_heads = lax.all_to_all(context_grad, "seq", split_axis=1, concat_axis=0, tiled=True)
         grad_heads = grad_heads.reshape(seq_slots, head_local, head_dim)
         qkv_head_grad = attention_backward(qkv_heads, log_total, grad_heads, seq_length)
-        qkv_grad = lax.all_to_all(
-            qkv_head_grad.reshape(seq_slots, 3, 1, head_local * head_dim),
-            "seq",
-            split_axis=0,
-            concat_axis=2,
-            tiled=True,
+        qkv_grad = jnp.concatenate(
+            lax.all_to_all(
+                jnp.stack(
+                    jnp.split(
+                        qkv_head_grad.reshape(seq_slots, 3, 1, head_local * head_dim),
+                        lax.axis_size("seq"),
+                        axis=0,
+                    )
+                ),
+                "seq",
+                0,
+                0,
+            ),
+            axis=2,
         )
         qkv_grad = qkv_grad.reshape(tok_rows, 3 * width)
         grad_qkv = matmul_left_t(inputs_mb, qkv_grad)

time: 971 us -> 916 us (0.943)
  waiting for transfers between devices: 215 us -> 181 us
  local copies, waits for them, and re-layouts: 112 us -> 89.6 us
    all_to_all x2, waiting for transfers between devices: 81 us -> 45.5 us  [on_device(): lax.all_to_all(jnp.stack(jnp.split(qkv_head_grad.reshape(seq_slots, 3, 1,...]
    all_to_all x4 -> x2, local copies, waits for them, and re-layouts: 17.7 us -> 3.57 us  [on_device(): lax.all_to_all(jnp.stack(jnp.split(qkv_head_grad.reshape(seq_slots, 3, 1,...]
  transfers between devices with their start and end apart: 17 -> 17, of which waited for: 7 -> 7; matrix products, arithmetic and copies ran while one was open for 55% -> 56% of each run, Pallas kernels for 0% -> 0%
where the time goes in v1:
time: 916 us; the launch traced here: 907 us
  matrix products  389 us (42%)
  waiting for transfers between devices  181 us (20%)
  other arithmetic  117 us (13%)
  local copies, waits for them, and re-layouts  89.6 us (10%)
  blocking collectives  73.3 us (8%)
  starting transfers between devices  40 us (4%)
  between operations  17.5 us (2%)
    dot_general x8, matrix products, matmul_plain(): return jnp.dot(left, right, preferred_element_type=jnp.float32)  66.5 us
    unnamed x10, waiting for transfers between devices  53.7 us
    dot_general x8, matrix products, one_block(): jnp.einsum('hqk,khd->qhd', grad_scores, key_rows, preferred_element_type=...  52.1 us
    unnamed x2, blocking collectives  51.4 us
    dot_general x8, matrix products, matmul_right_t(): lax.dot_general(left, right, (((1,), (1,)), ((), ())), preferred_element_...  47.6 us
    all_to_all x2, waiting for transfers between devices, on_device(): lax.all_to_all(jnp.stack(jnp.split(qkv_head_grad.reshape(seq_slots, 3, 1,...  45.5 us
    dot_general x8, matrix products, one_block(): jnp.einsum('hqk,qhd->khd', probs.astype(jnp.bfloat16), grad_block, prefer...  43.8 us
    all_to_all x2, waiting for transfers between devices, on_device(): lax.all_to_all(projected.reshape(tok_rows, 3, seq_devices, head_local * h...  43.4 us
  transfers between devices with their start and end apart: 17, of which 7 were waited for; matrix products, arithmetic and copies ran while one was open for 56% of the time, Pallas kernels for 0%

profile of v1, /device:TPU:0, one launch (start us, length us, event | category | flops | bytes accessed | tf_op | source)
XLA Modules:
  0.0 907.4 jit_solution(18021644476392049747)
XLA Ops:
  16.6 27.2 %all-reduce.18 = (bf16[768]{0:T(1024)(128)(2,1)S(1)}, bf16[768]{0:T(1024)(128)(2,1)S(1)}, bf16[768]{0:T(1024)(128)(2,1)}, bf16[768]{0:T(1024)(128)(2,1)}, bf16[7...) all-reduce(bf16[768]{0:T(1024)(128)(2,1)S(1)} %dynamic-update-slice, ...), channel_id=1, replica_groups=mesh['seq'=4,'shard'=8] {'shard'}, use_global_device_ids=true, to_apply=%add.1 | all-reduce | flops 6144 | bytes 24576
  46.7 5.7 fusion.104
  63.8 5.6 fusion.105
  76.9 39.0 %all-to-all-done = bf16[512,3,4,192]{0,3,1,2:T(8,128)(2,1)S(1)} async-done(((bf16[512,3,4,192]{0,3,1,2:T(8,128)(2,1)}), bf16[512,3,4,192]{0,3,1,2:T(8,128)(2,1)S(1)}, u32[]{:S(2)}, u32[]{:S(2)}) %all-to-all-start) | async-done | bytes 2359328 | tf_op jit(solution)/shard_map/all_to_all | solution.py:251
  123.9 5.9 reshape.321
  133.2 36.4 %while.56 = (s32[]{:T(128)}, bf16[4,512,3,64]{1,3,2,0:T(8,128)(2,1)}, f32[4,3,512]{2,1,0:T(4,128)S(1)}, bf16[4,512,3,64]{1,3,2,0:T(8,128)(2,1)S(1)}, bf16[2048,3...) while((s32[]{:T(128)}, ...), condition=%wide.region_3.4_spmd.clone, body=%wide.region_0.3_spmd.clone.sunk | while | flops 840008192 | bytes 39780960 | solution.py:124
  183.6 5.9 reshape.323
  192.1 34.0 %while.57 = (s32[]{:T(128)}, bf16[4,512,3,64]{1,3,2,0:T(8,128)(2,1)S(1)}, f32[4,3,512]{2,1,0:T(4,128)S(1)}, bf16[4,512,3,64]{1,3,2,0:T(8,128)(2,1)S(1)}, bf16[20...) while((s32[]{:T(128)}, ...), condition=%wide.region_11.12_spmd.clone, body=%wide.region_8.11_spmd.clone.sunk | while | flops 840008192 | bytes 39782500 | solution.py:124
  227.0 5.1 all-to-all-start.3
  232.7 8.8 all-gather
  255.0 5.0 fusion.144
  262.7 34.8 %multiply_convert_fusion.3 = (bf16[512,3072]{1,0:T(8,128)(2,1)}, f32[512,3072]{1,0:T(8,128)}, bf16[512,3072]{1,0:T(8,128)(2,1)}, f32[512,3072]{1,0:T(8,128)}, f32[512,3072]{1,0:T(8,128)}) fusion(f32[3072]{0:T(1024)S(1)} %bitcast.350, f32[512,3072]{1,0:T(8,128)S(1)} %fusion.144, bf16[768,3072]{1,0:T(8,128)(2,1)S(1)} %copy-done.66, ...), kind=kOutput, calls=%fused_computation.126 | convolution fusion | flops 2625503232 | bytes 37771264 | tf_op jit(solution)/shard_map/dot_general | solution.py:23
  297.5 6.2 fusion.163
  320.1 18.1 %convert_reduce_fusion.1 = (f32[3072]{0:T(1024)}, bf16[512,3072]{1,0:T(8,128)(2,1)}, f32[3072]{0:T(1024)}, bf16[512,3072]{1,0:T(8,128)(2,1)}) fusion(f32[512,3072]{1,0:T(8,128)} %get-tuple-element.614, f32[512,3072]{1,0:T(8,128)} %get-tuple-element.663, f32[3072]{0:T(1024)S(1)} %bitcast.351, f32[512,3072]{1,0:T(8,128)} %fusion.164, ...), kind=kOutput, calls=%fused_computation.110 | convolution fusion | flops 2469390336 | bytes 43290624 | tf_op jit(solution)/shard_map/dot_general | solution.py:33
  338.3 6.1 add_add_fusion.8
  344.4 6.4 multiply_reduce_fusion.3
  364.7 5.3 convolution_add_fusion
  379.8 9.0 fusion.146
  392.9 8.9 convolution_add_fusion.1
  401.8 5.3 all-to-all-start.6
  408.1 124.4 %while.58 = (s32[]{:T(128)}, f32[2048,3,64]{0,2,1:T(8,128)S(1)}, f32[2048,3,64]{0,2,1:T(8,128)}, bf16[4,512,3,64]{1,3,2,0:T(8,128)(2,1)}, bf16[4,512,3,64]{1,3,2...) while((s32[]{:T(128)}, f32[2048,3,64]{0,2,1:T(8,128)S(1)}, ...), condition=%wide.region_22.23_spmd.clone, body=%wide.region_20.22_spmd.clone.sunk | while | flops 2062516736 | bytes 204919504 | solution.py:171
  412.3 5.0 multiply_reduce_fusion.12
  427.3 7.0 fusion.275
  457.8 6.4 fusion.275
  464.2 5.7 fusion.274
  488.4 7.4 fusion.275
  495.8 5.9 fusion.274
  520.5 6.4 fusion.275
  526.9 5.6 fusion.274
  538.8 6.0 all-to-all-start.5
  545.7 120.8 %while.59 = (s32[]{:T(128)}, f32[2048,3,64]{0,2,1:T(8,128)S(1)}, f32[2048,3,64]{0,2,1:T(8,128)}, bf16[4,512,3,64]{1,3,2,0:T(8,128)(2,1)}, bf16[4,512,3,64]{1,3,2...) while((s32[]{:T(128)}, f32[2048,3,64]{0,2,1:T(8,128)S(1)}, ...), condition=%wide.region_29.30_spmd.clone, body=%wide.region_27.29_spmd.clone.sunk | while | flops 2062516736 | bytes 204919504 | solution.py:171
  564.3 6.2 fusion.288
  570.6 5.0 fusion.287
  594.0 6.3 fusion.288
  600.3 5.6 fusion.287
  624.4 6.2 fusion.288
  630.6 5.6 fusion.287
  654.7 6.3 fusion.288
  660.9 5.6 fusion.287
  672.7 5.0 all-to-all-start.7
  681.3 45.5 %all-to-all-done.7 = bf16[4,512,3,1,192]{1,4,2,3,0:T(8,128)(2,1)S(1)} async-done(((bf16[4,512,3,1,192]{1,4,2,3,0:T(8,128)(2,1)}), bf16[4,512,3,1,192]{1,4,2,3,0:T(8,128)(2,1)S(1)}, u32[]{:S(2)}, u32[]{:S(2)}) %all-to-all-start.7) | async-done | bytes 2359328 | tf_op jit(solution)/shard_map/all_to_all | solution.py:316
  731.9 5.0 add_bitcast_fusion
  736.9 8.0 copy.101
  758.1 51.0 %reduce-scatter.13.cloned.1.call-done = f32[96,2304]{1,0:T(8,128)} async-done(((f32[768,2304]{1,0:T(8,128)}), f32[96,2304]{1,0:T(8,128)}) %reduce-scatter.13.cloned.1.call-update) | async-done | bytes 884752
  812.0 24.3 %all-reduce.17 = (bf16[768]{0:T(1024)(128)(2,1)S(1)}, bf16[768]{0:T(1024)(128)(2,1)S(1)}, bf16[768]{0:T(1024)(128)(2,1)S(1)}, bf16[768]{0:T(1024)(128)(2,1)S(1)}...) all-reduce(f32[768]{0:T(1024)S(1)} %add.360, ...), channel_id=3, replica_groups=mesh['seq'=4,'shard'=8] {'shard'}, use_global_device_ids=true, to_apply=%region_34.35.clone | all-reduce | flops 9216 | bytes 55296
  837.0 13.0 %all-reduce.19 = (bf16[96]{0:T(256)(128)(2,1)S(1)}, bf16[96]{0:T(256)(128)(2,1)S(1)}, bf16[96]{0:T(256)(128)(2,1)S(1)}, bf16[96]{0:T(256)(128)(2,1)S(1)}, bf16[9...) all-reduce(bf16[96]{0:T(256)(128)(2,1)S(1)} %dynamic-slice.43, ...), channel_id=1, replica_groups=mesh['seq'=4,'shard'=8] {'seq'}, use_global_device_ids=true, to_apply=%region_35.36 | all-reduce | flops 1152 | bytes 4608 | tf_op jit(solution)/shard_map/psum | solution.py:369
  854.7 5.4 fusion.120
  863.6 30.5 %all-reduce.23.cloned.1.call-done = (bf16[96,2304]{0,1:T(8,128)(2,1)}, bf16[96,768]{1,0:T(8,128)(2,1)}, bf16[96,3072]{1,0:T(8,128)(2,1)}, bf16[384,768]{1,0:T(8,128)(2,1)}) async-done(((bf16[96,2304]{0,1:T(8,128)(2,1)}, bf16[96,768]{1,0:T(8,128)(2,1)}, bf16[96,3072]{1,0:T(8,128)(2,1)}, bf16[384,768]{1,0:T(8,128)(2,1)}), (bf16[96,2304]{0,1:T(8,128)(2,1)}, bf16[96,768]{1,0:T(8,128)(2,1)}, ...) | async-done | bytes 1769488 | tf_op jit(solution)/shard_map/psum | solution.py:368
  (439 shorter events, 391.4 us)
Async XLA Ops:
  7.2 39.5 %all-gather.6.cloned.1.call-start = ((), (), s32[]{:S(2)}) async-start(), calls=%async_computation.12 | async-start | bytes 3981312 | tf_op jit(solution)/shard_map/all_gather | solution.py:54
  57.0 59.0 %all-to-all-start = ((bf16[512,3,4,192]{0,3,1,2:T(8,128)(2,1)}), bf16[512,3,4,192]{0,3,1,2:T(8,128)(2,1)S(1)}, u32[]{:S(2)}, u32[]{:S(2)}) async-start(bf16[512,3,4,192]{0,3,1,2:T(8,128)(2,1)} %copy.83), calls=%async_computation | async-start | bytes 4718592 | tf_op jit(solution)/shard_map/all_to_all | solution.py:251
  61.7 181.3 %all-gather.8.cloned.1.call-start = ((), (), s32[]{:S(2)}) async-start(), calls=%async_computation.13 | async-start | bytes 1327104 | tf_op jit(solution)/shard_map/all_gather | solution.py:57
  62.4 192.6 %all-gather.10.cloned.1.call-start = ((), (), s32[]{:S(2)}) async-start(), calls=%async_computation.14 | async-start | bytes 5308416 | tf_op jit(solution)/shard_map/all_gather | solution.py:61
  115.9 58.1 %all-to-all-start.2 = ((bf16[512,3,4,192]{0,3,1,2:T(8,128)(2,1)}), bf16[512,3,4,192]{0,3,1,2:T(8,128)(2,1)}, u32[]{:S(2)}, u32[]{:S(2)}) async-start(bf16[512,3,4,192]{0,3,1,2:T(8,128)(2,1)} %copy.87), calls=%async_computation.2 | async-start | bytes 4718592 | tf_op jit(solution)/shard_map/all_to_all | solution.py:251
  169.6 13.9 %copy-start.6 = (bf16[2048,3,64]{0,2,1:T(8,128)(2,1)}, bf16[2048,3,64]{0,2,1:T(8,128)(2,1)S(1)}, u32[]{:S(2)}) copy-start(bf16[2048,3,64]{0,2,1:T(8,128)(2,1)S(1)} %get-tuple-element.1042) | copy-start | bytes 2359300
  169.6 13.9 %copy-start.11 = (bf16[2048,3,64]{0,2,1:T(8,128)(2,1)}, bf16[2048,3,64]{0,2,1:T(8,128)(2,1)S(1)}, u32[]{:S(2)}) copy-start(bf16[2048,3,64]{0,2,1:T(8,128)(2,1)S(1)} %get-tuple-element.1048) | copy-start | bytes 2359300
  169.6 13.9 %copy-start.14 = (bf16[4,512,3,64]{1,3,2,0:T(8,128)(2,1)}, bf16[4,512,3,64]{1,3,2,0:T(8,128)(2,1)S(1)}, u32[]{:S(2)}) copy-start(bf16[4,512,3,64]{1,3,2,0:T(8,128)(2,1)S(1)} %get-tuple-element.1053) | copy-start | bytes 2359300
  169.6 13.9 %copy-start.37 = (f32[4,3,512]{2,1,0:T(4,128)}, f32[4,3,512]{2,1,0:T(4,128)S(1)}, u32[]{:S(2)}) copy-start(f32[4,3,512]{2,1,0:T(4,128)S(1)} %get-tuple-element.995) | copy-start | bytes 73732
  174.1 52.1 %all-to-all-start.1 = ((bf16[4,512,192]{1,2,0:T(8,128)(2,1)}), bf16[4,512,192]{1,2,0:T(8,128)(2,1)}, u32[]{:S(2)}, u32[]{:S(2)}) async-start(bf16[4,512,192]{1,2,0:T(8,128)(2,1)} %bitcast.8), calls=%async_computation.1 | async-start | bytes 1572864 | tf_op jit(solution)/shard_map/all_to_all | solution.py:260
  192.0 40.6 %copy-start.63 = (bf16[768]{0:T(1024)(128)(2,1)S(1)}, bf16[768]{0:T(1024)(128)(2,1)}, u32[]{:S(2)}) copy-start(bf16[768]{0:T(1024)(128)(2,1)} %get-tuple-element.570) | copy-start | bytes 4612
  192.1 40.6 %copy-start.62 = (bf16[768]{0:T(1024)(128)(2,1)S(1)}, bf16[768]{0:T(1024)(128)(2,1)}, u32[]{:S(2)}) copy-start(bf16[768]{0:T(1024)(128)(2,1)} %get-tuple-element.572) | copy-start | bytes 4612
  192.1 40.6 %copy-start.61 = (bf16[768]{0:T(1024)(128)(2,1)S(1)}, bf16[768]{0:T(1024)(128)(2,1)}, u32[]{:S(2)}) copy-start(bf16[768]{0:T(1024)(128)(2,1)} %get-tuple-element.571) | copy-start | bytes 4612
  192.1 40.6 %copy-start.65 = (bf16[384]{0:T(512)(128)(2,1)S(1)}, bf16[384]{0:T(512)(128)(2,1)}, u32[]{:S(2)}) copy-start(bf16[384]{0:T(512)(128)(2,1)} %param.34) | copy-start | bytes 2308
  192.1 49.5 %copy-start.60 = (bf16[768]{0:T(1024)(128)(2,1)S(1)}, bf16[768]{0:T(1024)(128)(2,1)}, u32[]{:S(2)}) copy-start(bf16[768]{0:T(1024)(128)(2,1)} %get-tuple-element.573) | copy-start | bytes 4612
  192.1 49.5 %copy-start.59 = (bf16[768]{0:T(1024)(128)(2,1)S(1)}, bf16[768]{0:T(1024)(128)(2,1)}, u32[]{:S(2)}) copy-start(bf16[768]{0:T(1024)(128)(2,1)} %get-tuple-element.574) | copy-start | bytes 4612
  192.1 49.5 %copy-start.58 = (bf16[768]{0:T(1024)(128)(2,1)S(1)}, bf16[768]{0:T(1024)(128)(2,1)}, u32[]{:S(2)}) copy-start(bf16[768]{0:T(1024)(128)(2,1)} %get-tuple-element.575) | copy-start | bytes 4612
  226.1 20.7 %copy-start.4 = (bf16[2048,3,64]{0,2,1:T(8,128)(2,1)}, bf16[2048,3,64]{0,2,1:T(8,128)(2,1)S(1)}, u32[]{:S(2)}) copy-start(bf16[2048,3,64]{0,2,1:T(8,128)(2,1)S(1)} %get-tuple-element.1041) | copy-start | bytes 2359300
  226.1 20.7 %copy-start.9 = (bf16[2048,3,64]{0,2,1:T(8,128)(2,1)}, bf16[2048,3,64]{0,2,1:T(8,128)(2,1)S(1)}, u32[]{:S(2)}) copy-start(bf16[2048,3,64]{0,2,1:T(8,128)(2,1)S(1)} %get-tuple-element.1047) | copy-start | bytes 2359300
  226.1 20.7 %copy-start.13 = (bf16[4,512,3,64]{1,3,2,0:T(8,128)(2,1)}, bf16[4,512,3,64]{1,3,2,0:T(8,128)(2,1)S(1)}, u32[]{:S(2)}) copy-start(bf16[4,512,3,64]{1,3,2,0:T(8,128)(2,1)S(1)} %get-tuple-element.1052) | copy-start | bytes 2359300
  226.1 20.7 %copy-start.38 = (f32[4,3,512]{2,1,0:T(4,128)}, f32[4,3,512]{2,1,0:T(4,128)S(1)}, u32[]{:S(2)}) copy-start(f32[4,3,512]{2,1,0:T(4,128)S(1)} %get-tuple-element.959) | copy-start | bytes 73732
  227.0 24.2 %all-to-all-start.3 = ((bf16[4,512,192]{1,2,0:T(8,128)(2,1)}), bf16[4,512,192]{1,2,0:T(8,128)(2,1)S(1)}, u32[]{:S(2)}, u32[]{:S(2)}) async-start(bf16[4,512,192]{1,2,0:T(8,128)(2,1)} %bitcast.341), calls=%async_computation.3 | async-start | bytes 1572864 | tf_op jit(solution)/shard_map/all_to_all | solution.py:260
  232.0 65.4 %all-gather.12.cloned.1.call-start = ((), (), s32[]{:S(2)}) async-start(), calls=%async_computation.15 | async-start | bytes 5308416 | tf_op jit(solution)/shard_map/all_gather | solution.py:63
  232.6 516.5 %reduce-scatter.7.cloned.1.call-start = ((), (), s32[]{:S(2)}) async-start(), calls=%async_computation.16 | async-start | bytes 2654208 | tf_op jit(solution)/shard_map/reduce_scatter | solution.py:356
  255.0 7.6 copy-start.66
  359.8 393.6 %reduce-scatter.11.cloned.1.call-start = ((), (), s32[]{:S(2)}) async-start(), calls=%async_computation.18 | async-start | bytes 10616832 | tf_op jit(solution)/shard_map/reduce_scatter | solution.py:362
  375.6 26.2 %all-to-all-start.4 = ((bf16[512,4,192]{0,2,1:T(8,128)(2,1)}), bf16[512,4,192]{0,2,1:T(8,128)(2,1)}, u32[]{:S(2)}, u32[]{:S(2)}) async-start(bf16[512,4,192]{0,2,1:T(8,128)(2,1)} %bitcast.340), calls=%async_computation.4 | async-start | bytes 1572864 | tf_op jit(solution)/shard_map/all_to_all | solution.py:312
  379.8 376.0 %reduce-scatter.9.cloned.1.call-start = ((), (), s32[]{:S(2)}) async-start(), calls=%async_computation.17 | async-start | bytes 10616832 | tf_op jit(solution)/shard_map/reduce_scatter | solution.py:360
  379.8 9.0 copy-start.29
  379.8 9.0 copy-start.69
  401.8 137.0 %all-to-all-start.6 = ((bf16[512,4,192]{0,2,1:T(8,128)(2,1)}), bf16[512,4,192]{0,2,1:T(8,128)(2,1)}, u32[]{:S(2)}, u32[]{:S(2)}) async-start(bf16[512,4,192]{0,2,1:T(8,128)(2,1)} %bitcast.339), calls=%async_computation.6 | async-start | bytes 1572864 | tf_op jit(solution)/shard_map/all_to_all | solution.py:312
  410.9 7.1 copy-start
  422.9 11.4 %copy-start.1 = (f32[3,512,2048]{2,1,0:T(8,128)S(1)}, f32[3,512,2048]{2,1,0:T(8,128)}, u32[]{:S(2)}) copy-start(f32[3,512,2048]{2,1,0:T(8,128)} %copy-done) | copy-start | bytes 37748740 | tf_op jit(solution)/shard_map/while
  453.4 10.8 %copy-start.1 = (f32[3,512,2048]{2,1,0:T(8,128)S(1)}, f32[3,512,2048]{2,1,0:T(8,128)}, u32[]{:S(2)}) copy-start(f32[3,512,2048]{2,1,0:T(8,128)} %copy-done) | copy-start | bytes 37748740 | tf_op jit(solution)/shard_map/while
  484.0 11.8 %copy-start.1 = (f32[3,512,2048]{2,1,0:T(8,128)S(1)}, f32[3,512,2048]{2,1,0:T(8,128)}, u32[]{:S(2)}) copy-start(f32[3,512,2048]{2,1,0:T(8,128)} %copy-done) | copy-start | bytes 37748740 | tf_op jit(solution)/shard_map/while
  515.8 11.1 %copy-start.1 = (f32[3,512,2048]{2,1,0:T(8,128)S(1)}, f32[3,512,2048]{2,1,0:T(8,128)}, u32[]{:S(2)}) copy-start(f32[3,512,2048]{2,1,0:T(8,128)} %copy-done) | copy-start | bytes 37748740 | tf_op jit(solution)/shard_map/while
  538.8 6.9 copy-start.5
  538.8 6.9 copy-start.8
  538.8 6.9 copy-start.10
  538.8 134.0 %all-to-all-start.5 = ((bf16[4,512,3,1,192]{1,4,2,3,0:T(8,128)(2,1)}), bf16[4,512,3,1,192]{1,4,2,3,0:T(8,128)(2,1)}, u32[]{:S(2)}, u32[]{:S(2)}) async-start(bf16[4,512,3,1,192]{1,4,2,3,0:T(8,128)(2,1)} %pad_maximum_fusion.1), calls=%async_computation.5 | async-start | bytes 4718592 | tf_op jit(solution)/shard_map/all_to_all | solution.py:316
  559.8 10.8 %copy-start.3 = (f32[3,512,2048]{2,1,0:T(8,128)S(1)}, f32[3,512,2048]{2,1,0:T(8,128)}, u32[]{:S(2)}) copy-start(f32[3,512,2048]{2,1,0:T(8,128)} %copy-done.2) | copy-start | bytes 37748740 | tf_op jit(solution)/shard_map/while
  589.6 10.7 %copy-start.3 = (f32[3,512,2048]{2,1,0:T(8,128)S(1)}, f32[3,512,2048]{2,1,0:T(8,128)}, u32[]{:S(2)}) copy-start(f32[3,512,2048]{2,1,0:T(8,128)} %copy-done.2) | copy-start | bytes 37748740 | tf_op jit(solution)/shard_map/while
  620.0 10.7 %copy-start.3 = (f32[3,512,2048]{2,1,0:T(8,128)S(1)}, f32[3,512,2048]{2,1,0:T(8,128)}, u32[]{:S(2)}) copy-start(f32[3,512,2048]{2,1,0:T(8,128)} %copy-done.2) | copy-start | bytes 37748740 | tf_op jit(solution)/shard_map/while
  650.3 10.7 %copy-start.3 = (f32[3,512,2048]{2,1,0:T(8,128)S(1)}, f32[3,512,2048]{2,1,0:T(8,128)}, u32[]{:S(2)}) copy-start(f32[3,512,2048]{2,1,0:T(8,128)} %copy-done.2) | copy-start | bytes 37748740 | tf_op jit(solution)/shard_map/while
  672.7 54.1 %all-to-all-start.7 = ((bf16[4,512,3,1,192]{1,4,2,3,0:T(8,128)(2,1)}), bf16[4,512,3,1,192]{1,4,2,3,0:T(8,128)(2,1)S(1)}, u32[]{:S(2)}, u32[]{:S(2)}) async-start(bf16[4,512,3,1,192]{1,4,2,3,0:T(8,128)(2,1)} %pad_maximum_fusion.3), calls=%async_computation.7 | async-start | bytes 4718592 | tf_op jit(solution)/shard_map/all_to_all | solution.py:316
  677.8 131.4 %reduce-scatter.13.cloned.1.call-start = ((), (), s32[]{:S(2)}) async-start(), calls=%async_computation.19 | async-start | bytes 7962624
  745.0 149.1 %all-reduce.23.cloned.1.call-start = ((), (), s32[]{:S(2)}) async-start(), calls=%async_computation.20 | async-start | bytes 3833856 | tf_op jit(solution)/shard_map/psum | solution.py:368
  758.1 96.6 %copy-start.51 = (f32[512]{0:T(512)S(1)}, f32[512]{0:T(512)}, u32[]{:S(2)}) copy-start(f32[512]{0:T(512)} %copy-done.50) | copy-start | bytes 6148
  (54 other events, 203.7 us)
Sparse Core Ops, SparseCore 0:
  9.9 36.7 all-gather.5
  64.4 24.3 all-gather.7
  90.7 38.7 all-gather.9
  234.4 39.2 all-gather.11
  359.9 40.3 reduce-scatter.6
  403.7 76.8 reduce-scatter.10
  484.1 76.8 reduce-scatter.8
  745.1 63.9 reduce-scatter.12
  812.9 81.1 all-reduce.22
